TPU v7x, 32 devices: a whole 2x2x4 slice. The times are simulated.
32 devices in a mesh: row: 8 (over y, x, core), col: 4 (over z).
Axes of the slice: x: 2, y: 2, z: 4, core: 2. Of those that a mesh axis runs over, the one named last changes fastest.
Arguments:
- factor_a: bfloat16 [128, 32768], P('row', 'col'), may hold values from -12 to 12
- factor_b: bfloat16 [128, 32768], P('row', 'col'), may hold values from -12 to 12
- pair: bfloat16 [1024, 1024, 128], P('row', 'col'), may hold values from -6 to 6
- proj_weight: bfloat16 [1024, 128], replicated, may hold values from -0.1875 to 0.1875
- proj_bias: float32 [128], replicated, may hold values from -3 to 3
- norm_gain: float32 [128], replicated, may hold values from 0.25 to 1.75
- norm_bias: float32 [128], replicated, may hold values from -3 to 3
- trans_in: bfloat16 [128, 1024], replicated, may hold values from -0.5 to 0.5
- trans_out: bfloat16 [512, 128], replicated, may hold values from -0.25 to 0.25
- cotangent: bfloat16 [1024, 1024, 128], P('row', 'col'), may hold values from -6 to 6
Outputs:
- new_pair: bfloat16 [1024, 1024, 128], P('row', 'col')
- pair_grad: bfloat16 [1024, 1024, 128], P('row', 'col')
- grad_a: float32 [128, 32768], P('row', 'col')
- grad_b: float32 [128, 32768], P('row', 'col')
All inputs are finite; a program needn't handle non-finite values.
Results may differ from a plain program's by a relative error of at most 0.006.
Values may be sent and summed in bfloat16 or wider, within the bound.
No kernel may reach another device: no remote copies, remote signals or barrier semaphores. Data moves between devices by JAX's collectives and lax.ppermute only.
A program may use at most 128 MiB of HBM per device.

v0:
```python
import jax
import jax.numpy as jnp
from jax import lax
from jax.sharding import PartitionSpec as P

H = 32


def dot_last(left, right):
    return lax.dot_general(
        left, right, (((1,), (1,)), ((), ())), preferred_element_type=jnp.float32
    )


def dot_first(left, right):
    return lax.dot_general(
        left, right, (((0,), (0,)), ((), ())), preferred_element_type=jnp.float32
    )


def factor_pull(grad_rows, proj_weight, seq_count, hidden_dim):
    rows_i, cols_j, width = grad_rows.shape
    weight_cube = proj_weight.reshape(hidden_dim, hidden_dim, width)
    pulled = (
        jnp.einsum("abc,hkc->ahbk", grad_rows, weight_cube, preferred_element_type=jnp.float32)
        / seq_count
    )
    pulled = pulled.astype(jnp.bfloat16)
    return pulled.reshape(rows_i * hidden_dim, cols_j * hidden_dim)


def pair_update(
    a_block,
    b_cols,
    pair_rows,
    cot_rows,
    proj_weight,
    proj_bias,
    norm_gain,
    norm_bias,
    trans_in,
    trans_out,
    seq_count,
    hidden_dim,
):
    rows_i, cols_j, width = pair_rows.shape
    units = trans_out.shape[0]
    outer = (dot_first(a_block, b_cols) / seq_count).astype(jnp.bfloat16)
    outer = outer.reshape(rows_i, hidden_dim, cols_j, hidden_dim)
    weight_cube = proj_weight.reshape(hidden_dim, hidden_dim, width)
    projected = jnp.einsum("ahbk,hkc->abc", outer, weight_cube, preferred_element_type=jnp.float32)
    updated = pair_rows.reshape(rows_i * cols_j, width).astype(jnp.float32)
    updated = updated + projected.reshape(rows_i * cols_j, width) + proj_bias
    row_mean = jnp.mean(updated, axis=-1, keepdims=True)
    centered = updated - row_mean
    row_var = jnp.mean(centered * centered, axis=-1, keepdims=True)
    inv_std = lax.rsqrt(row_var + 1e-05)
    normed = centered * inv_std
    lnorm = (normed * norm_gain + norm_bias).astype(jnp.bfloat16)
    both_pre = jnp.dot(lnorm, trans_in, preferred_element_type=jnp.float32)
    gate_pre = both_pre[:, :units]
    up_pre = both_pre[:, units:]
    sig_gate = jax.nn.sigmoid(gate_pre)
    activated = gate_pre * sig_gate
    hidden = (activated * up_pre).astype(jnp.bfloat16)
    new_rows = (updated + jnp.dot(hidden, trans_out, preferred_element_type=jnp.float32)).astype(
        jnp.bfloat16
    )
    cot_flat = cot_rows.reshape(rows_i * cols_j, width)
    d_hidden = dot_last(cot_flat, trans_out)
    d_gate = d_hidden * up_pre * sig_gate * (1.0 + gate_pre * (1.0 - sig_gate))
    d_up = d_hidden * activated
    d_both = jnp.concatenate([d_gate, d_up], axis=-1).astype(jnp.bfloat16)
    d_norm = dot_last(d_both, trans_in) * norm_gain
    d_mean = jnp.mean(d_norm, axis=-1, keepdims=True)
    d_proj = jnp.mean(d_norm * normed, axis=-1, keepdims=True)
    grad_flat = cot_flat.astype(jnp.float32) + inv_std * (d_norm - d_mean - normed * d_proj)
    grad_rows = grad_flat.astype(jnp.bfloat16).reshape(rows_i, cols_j, width)
    pulled = factor_pull(grad_rows, proj_weight, seq_count, hidden_dim)
    return (new_rows.reshape(rows_i, cols_j, width), grad_rows, pulled)


def pick_rows(rows_here, cols_here):
    target = max(8, 1024 // cols_here)
    block_rows = 8
    for candidate in range(8, rows_here + 1, 8):
        if rows_here % candidate == 0 and candidate <= target:
            block_rows = candidate
    return block_rows


def body(
    factor_a,
    factor_b,
    pair,
    proj_weight,
    proj_bias,
    norm_gain,
    norm_bias,
    trans_in,
    trans_out,
    cotangent,
):
    rows_here, cols_here, width = pair.shape
    seq_count = factor_a.shape[0] * lax.axis_size("row")
    block_rows = pick_rows(rows_here, cols_here)
    blocks = rows_here // block_rows
    gathered = lax.all_gather(factor_a, "col", axis=1, tiled=True)
    own_rows = lax.all_to_all(gathered, "row", split_axis=1, concat_axis=0, tiled=True)
    b_cols = lax.all_gather(factor_b, "row", axis=0, tiled=True)
    a_blocks = own_rows.reshape(seq_count, blocks, block_rows * H).transpose(1, 0, 2)
    pair_blocks = pair.reshape(blocks, block_rows, cols_here, width)
    cot_blocks = cotangent.reshape(blocks, block_rows, cols_here, width)

    def one_block(inputs_now):
        a_block, pair_rows, cot_rows = inputs_now
        new_rows, grad_rows, pulled = pair_update(
            a_block,
            b_cols,
            pair_rows,
            cot_rows,
            proj_weight,
            proj_bias,
            norm_gain,
            norm_bias,
            trans_in,
            trans_out,
            seq_count,
            H,
        )
        grad_a_block = dot_last(b_cols, pulled)
        return (new_rows, grad_rows, grad_a_block, pulled, a_block)

    def advance_sum(running, inputs_now):
        new_rows, grad_rows, grad_a_block, pulled, a_block = one_block(inputs_now)
        running = running + jnp.dot(a_block, pulled, preferred_element_type=jnp.float32)
        return (running, (new_rows, grad_rows, grad_a_block))

    start_sum = jnp.zeros((seq_count, cols_here * H), jnp.float32)
    column_sum, outputs = lax.scan(advance_sum, start_sum, (a_blocks, pair_blocks, cot_blocks))
    new_stack, grad_stack, part_stack = outputs
    grad_b = lax.psum_scatter(column_sum, "row", scatter_dimension=0, tiled=True)
    new_pair = new_stack.reshape(rows_here, cols_here, width)
    pair_grad = grad_stack.reshape(rows_here, cols_here, width)
    grad_a_part = part_stack.transpose(1, 0, 2).reshape(seq_count, rows_here * H)
    returned = lax.all_to_all(grad_a_part, "row", split_axis=0, concat_axis=1, tiled=True)
    grad_a = lax.psum_scatter(returned, "col", scatter_dimension=1, tiled=True)
    return (new_pair, pair_grad, grad_a, grad_b)


def solution(mesh):
    placed = (
        P("row", "col"),
        P("row", "col"),
        P("row", "col", None),
        P(),
        P(),
        P(),
        P(),
        P(),
        P(),
        P("row", "col", None),
    )
    return jax.shard_map(
        body,
        mesh=mesh,
        in_specs=placed,
        out_specs=(P("row", "col", None), P("row", "col", None), P("row", "col"), P("row", "col")),
        check_vma=False,
    )
```

profile of v0, /device:TPU:0, one launch (start us, length us, event | category | flops | bytes accessed | tf_op | source)
XLA Modules:
  0.0 1988.5 jit_solution(11511176603464215698)
XLA Ops:
  8.6 31.6 %all-gather.3.cloned.1.call-done = bf16[16,32768]{1,0:T(8,128)(2,1)} async-done(((bf16[16,8192]{1,0:T(8,128)(2,1)}), bf16[16,32768]{1,0:T(8,128)(2,1)}) %all-gather.3.cloned.1.call-update) | async-done | bytes 1048592 | tf_op jit(solution)/shard_map/all_gather | solution.py:108
  46.4 18.1 all-to-all-done
  75.1 1774.4 %while.17 = (s32[]{:T(128)}, f32[128,8192]{1,0:T(8,128)}, bf16[16,8,256,128]{3,2,1,0:T(8,128)(2,1)}, bf16[16,8,256,128]{3,2,1,0:T(8,128)(2,1)}, f32[16,128,256]{...) while((s32[]{:T(128)}, f32[128,8192]{1,0:T(8,128)}, ...), condition=%wide.region_5.6_spmd.clone, body=%wide.region_0.5_spmd.clone.sunk | while | flops 4341368832 | bytes 152742176 | solution.py:140
  82.2 17.3 reshape.98
  99.5 15.4 copy.34
  153.7 21.9 %reshape.99 = bf16[256,8192]{1,0:T(8,128)(2,1)} reshape(bf16[8,32,256,32]{3,2,1,0:T(8,128)(2,1)} %copy.35) | data formatting | bytes 8388608 | tf_op jit(solution)/shard_map/while/body/eval_jaxpr/reshape | solution.py:29
  191.8 17.3 reshape.98
  209.1 15.4 copy.34
  263.3 21.9 %reshape.99 = bf16[256,8192]{1,0:T(8,128)(2,1)} reshape(bf16[8,32,256,32]{3,2,1,0:T(8,128)(2,1)} %copy.35) | data formatting | bytes 8388608 | tf_op jit(solution)/shard_map/while/body/eval_jaxpr/reshape | solution.py:29
  302.8 17.3 reshape.98
  320.1 15.4 copy.34
  374.3 21.9 %reshape.99 = bf16[256,8192]{1,0:T(8,128)(2,1)} reshape(bf16[8,32,256,32]{3,2,1,0:T(8,128)(2,1)} %copy.35) | data formatting | bytes 8388608 | tf_op jit(solution)/shard_map/while/body/eval_jaxpr/reshape | solution.py:29
  413.8 17.3 reshape.98
  431.0 15.4 copy.34
  485.3 21.9 %reshape.99 = bf16[256,8192]{1,0:T(8,128)(2,1)} reshape(bf16[8,32,256,32]{3,2,1,0:T(8,128)(2,1)} %copy.35) | data formatting | bytes 8388608 | tf_op jit(solution)/shard_map/while/body/eval_jaxpr/reshape | solution.py:29
  524.8 17.3 reshape.98
  542.0 15.4 copy.34
  596.3 21.9 %reshape.99 = bf16[256,8192]{1,0:T(8,128)(2,1)} reshape(bf16[8,32,256,32]{3,2,1,0:T(8,128)(2,1)} %copy.35) | data formatting | bytes 8388608 | tf_op jit(solution)/shard_map/while/body/eval_jaxpr/reshape | solution.py:29
  635.7 17.3 reshape.98
  653.0 15.4 copy.34
  707.3 21.9 %reshape.99 = bf16[256,8192]{1,0:T(8,128)(2,1)} reshape(bf16[8,32,256,32]{3,2,1,0:T(8,128)(2,1)} %copy.35) | data formatting | bytes 8388608 | tf_op jit(solution)/shard_map/while/body/eval_jaxpr/reshape | solution.py:29
  746.7 17.3 reshape.98
  764.0 15.4 copy.34
  818.3 21.9 %reshape.99 = bf16[256,8192]{1,0:T(8,128)(2,1)} reshape(bf16[8,32,256,32]{3,2,1,0:T(8,128)(2,1)} %copy.35) | data formatting | bytes 8388608 | tf_op jit(solution)/shard_map/while/body/eval_jaxpr/reshape | solution.py:29
  857.7 17.3 reshape.98
  875.0 15.4 copy.34
  929.3 21.9 %reshape.99 = bf16[256,8192]{1,0:T(8,128)(2,1)} reshape(bf16[8,32,256,32]{3,2,1,0:T(8,128)(2,1)} %copy.35) | data formatting | bytes 8388608 | tf_op jit(solution)/shard_map/while/body/eval_jaxpr/reshape | solution.py:29
  968.7 17.3 reshape.98
  1040.2 21.9 %reshape.99 = bf16[256,8192]{1,0:T(8,128)(2,1)} reshape(bf16[8,32,256,32]{3,2,1,0:T(8,128)(2,1)} %copy.35) | data formatting | bytes 8388608 | tf_op jit(solution)/shard_map/while/body/eval_jaxpr/reshape | solution.py:29
  1079.7 17.3 reshape.98
  1151.2 21.9 %reshape.99 = bf16[256,8192]{1,0:T(8,128)(2,1)} reshape(bf16[8,32,256,32]{3,2,1,0:T(8,128)(2,1)} %copy.35) | data formatting | bytes 8388608 | tf_op jit(solution)/shard_map/while/body/eval_jaxpr/reshape | solution.py:29
  1190.7 17.3 reshape.98
  1207.9 15.4 copy.34
  1262.2 21.9 %reshape.99 = bf16[256,8192]{1,0:T(8,128)(2,1)} reshape(bf16[8,32,256,32]{3,2,1,0:T(8,128)(2,1)} %copy.35) | data formatting | bytes 8388608 | tf_op jit(solution)/shard_map/while/body/eval_jaxpr/reshape | solution.py:29
  1301.7 17.3 reshape.98
  1373.2 21.9 %reshape.99 = bf16[256,8192]{1,0:T(8,128)(2,1)} reshape(bf16[8,32,256,32]{3,2,1,0:T(8,128)(2,1)} %copy.35) | data formatting | bytes 8388608 | tf_op jit(solution)/shard_map/while/body/eval_jaxpr/reshape | solution.py:29
  1412.6 17.3 reshape.98
  1484.2 21.9 %reshape.99 = bf16[256,8192]{1,0:T(8,128)(2,1)} reshape(bf16[8,32,256,32]{3,2,1,0:T(8,128)(2,1)} %copy.35) | data formatting | bytes 8388608 | tf_op jit(solution)/shard_map/while/body/eval_jaxpr/reshape | solution.py:29
  1523.6 17.3 reshape.98
  1595.2 21.9 %reshape.99 = bf16[256,8192]{1,0:T(8,128)(2,1)} reshape(bf16[8,32,256,32]{3,2,1,0:T(8,128)(2,1)} %copy.35) | data formatting | bytes 8388608 | tf_op jit(solution)/shard_map/while/body/eval_jaxpr/reshape | solution.py:29
  1634.6 17.3 reshape.98
  1651.9 15.4 copy.34
  1706.2 21.9 %reshape.99 = bf16[256,8192]{1,0:T(8,128)(2,1)} reshape(bf16[8,32,256,32]{3,2,1,0:T(8,128)(2,1)} %copy.35) | data formatting | bytes 8388608 | tf_op jit(solution)/shard_map/while/body/eval_jaxpr/reshape | solution.py:29
  1745.6 17.3 reshape.98
  1817.1 21.9 %reshape.99 = bf16[256,8192]{1,0:T(8,128)(2,1)} reshape(bf16[8,32,256,32]{3,2,1,0:T(8,128)(2,1)} %copy.35) | data formatting | bytes 8388608 | tf_op jit(solution)/shard_map/while/body/eval_jaxpr/reshape | solution.py:29
  1853.3 30.1 %all_to_all.35 = f32[8,16,4096]{2,1,0:T(8,128)S(1)} all-to-all(f32[8,16,4096]{2,1,0:T(8,128)} %all_to_all.29), channel_id=1, replica_groups=mesh['row'=8,'col'=4] {'row'}, dimensions={0} | all-to-all | bytes 4194304 | tf_op jit(solution)/shard_map/all_to_all | solution.py:146
  1885.5 42.3 %reduce-scatter.3.cloned.1.call-done = f32[16,8192]{1,0:T(8,128)} async-done(((f32[16,32768]{1,0:T(8,128)}), f32[16,8192]{1,0:T(8,128)}) %reduce-scatter.3.cloned.1.call-update) | async-done | bytes 524304 | tf_op jit(solution)/shard_map/reduce_scatter | solution.py:147
  1927.8 54.2 %reduce-scatter.5.cloned.1.call-done = f32[16,8192]{1,0:T(8,128)} async-done(((f32[128,8192]{1,0:T(8,128)}), f32[16,8192]{1,0:T(8,128)}) %reduce-scatter.5.cloned.1.call-update) | async-done | bytes 524304 | tf_op jit(solution)/shard_map/reduce_scatter | solution.py:142
  (454 shorter events, 1016.4 us)
Async XLA Ops:
  7.2 33.1 %all-gather.3.cloned.1.call-start = ((), (), s32[]{:S(2)}) async-start(), calls=%async_computation.4 | async-start | bytes 1310720 | tf_op jit(solution)/shard_map/all_gather | solution.py:108
  7.9 67.2 %all-gather.5.cloned.1.call-start = ((), (), s32[]{:S(2)}) async-start(), calls=%async_computation.5 | async-start | bytes 2359296 | tf_op jit(solution)/shard_map/all_gather | solution.py:110
  40.3 34.8 %copy-start.2 = (bf16[128,1024]{1,0:T(8,128)(2,1)S(1)}, bf16[128,1024]{1,0:T(8,128)(2,1)}, u32[]{:S(2)}) copy-start(bf16[128,1024]{1,0:T(8,128)(2,1)} %param.19) | copy-start | bytes 786436
  40.3 34.8 %copy-start.3 = (bf16[1024,128]{1,0:T(8,128)(2,1)S(1)}, bf16[1024,128]{1,0:T(8,128)(2,1)}, u32[]{:S(2)}) copy-start(bf16[1024,128]{1,0:T(8,128)(2,1)} %param.15) | copy-start | bytes 786436
  40.3 34.8 %copy-start.5 = (f32[128]{0:T(128)S(1)}, f32[128]{0:T(128)}, u32[]{:S(2)}) copy-start(f32[128]{0:T(128)} %param.17) | copy-start | bytes 1540
  40.3 34.8 %copy-start.6 = (f32[128]{0:T(128)S(1)}, f32[128]{0:T(128)}, u32[]{:S(2)}) copy-start(f32[128]{0:T(128)} %param.18) | copy-start | bytes 1540
  40.3 34.8 %copy-start.7 = (bf16[512,128]{1,0:T(8,128)(2,1)S(1)}, bf16[512,128]{1,0:T(8,128)(2,1)}, u32[]{:S(2)}) copy-start(bf16[512,128]{1,0:T(8,128)(2,1)} %param.20) | copy-start | bytes 393220
  40.3 34.8 %copy-start.8 = (f32[128]{0:T(128)S(1)}, f32[128]{0:T(128)}, u32[]{:S(2)}) copy-start(f32[128]{0:T(128)} %param.16) | copy-start | bytes 1540
  42.6 21.8 %all-to-all-start = ((bf16[16,8,4096]{2,0,1:T(8,128)(2,1)}), bf16[16,8,4096]{2,0,1:T(8,128)(2,1)S(1)}, u32[]{:S(2)}, u32[]{:S(2)}) async-start(bf16[16,8,4096]{2,0,1:T(8,128)(2,1)} %bitcast.70), calls=%async_computation | async-start | bytes 2097152 | tf_op jit(solution)/shard_map/all_to_all | solution.py:109
  46.3 1881.5 %reduce-scatter.3.cloned.1.call-start = ((), (), s32[]{:S(2)}) async-start(), calls=%async_computation.6 | async-start | bytes 2621440 | tf_op jit(solution)/shard_map/reduce_scatter | solution.py:147
  153.7 21.9 %copy-start.1 = (bf16[128,8192]{1,0:T(8,128)(2,1)S(1)}, bf16[128,8192]{1,0:T(8,128)(2,1)}, u32[]{:S(2)}) copy-start(bf16[128,8192]{1,0:T(8,128)(2,1)} %get-tuple-element.356) | copy-start | bytes 6291460 | tf_op jit(solution)/shard_map/while
  175.6 4.3 copy-start
  179.9 4.9 copy-start.4
  263.3 21.9 %copy-start.1 = (bf16[128,8192]{1,0:T(8,128)(2,1)S(1)}, bf16[128,8192]{1,0:T(8,128)(2,1)}, u32[]{:S(2)}) copy-start(bf16[128,8192]{1,0:T(8,128)(2,1)} %get-tuple-element.356) | copy-start | bytes 6291460 | tf_op jit(solution)/shard_map/while
  289.5 6.3 copy-start.4
  374.3 21.9 %copy-start.1 = (bf16[128,8192]{1,0:T(8,128)(2,1)S(1)}, bf16[128,8192]{1,0:T(8,128)(2,1)}, u32[]{:S(2)}) copy-start(bf16[128,8192]{1,0:T(8,128)(2,1)} %get-tuple-element.356) | copy-start | bytes 6291460 | tf_op jit(solution)/shard_map/while
  400.4 6.3 copy-start.4
  485.3 21.9 %copy-start.1 = (bf16[128,8192]{1,0:T(8,128)(2,1)S(1)}, bf16[128,8192]{1,0:T(8,128)(2,1)}, u32[]{:S(2)}) copy-start(bf16[128,8192]{1,0:T(8,128)(2,1)} %get-tuple-element.356) | copy-start | bytes 6291460 | tf_op jit(solution)/shard_map/while
  507.2 4.3 copy-start
  511.5 6.3 copy-start.4
  596.3 21.9 %copy-start.1 = (bf16[128,8192]{1,0:T(8,128)(2,1)S(1)}, bf16[128,8192]{1,0:T(8,128)(2,1)}, u32[]{:S(2)}) copy-start(bf16[128,8192]{1,0:T(8,128)(2,1)} %get-tuple-element.356) | copy-start | bytes 6291460 | tf_op jit(solution)/shard_map/while
  622.4 6.3 copy-start.4
  707.3 21.9 %copy-start.1 = (bf16[128,8192]{1,0:T(8,128)(2,1)S(1)}, bf16[128,8192]{1,0:T(8,128)(2,1)}, u32[]{:S(2)}) copy-start(bf16[128,8192]{1,0:T(8,128)(2,1)} %get-tuple-element.356) | copy-start | bytes 6291460 | tf_op jit(solution)/shard_map/while
  729.2 4.2 copy-start
  733.4 6.3 copy-start.4
  818.3 21.9 %copy-start.1 = (bf16[128,8192]{1,0:T(8,128)(2,1)S(1)}, bf16[128,8192]{1,0:T(8,128)(2,1)}, u32[]{:S(2)}) copy-start(bf16[128,8192]{1,0:T(8,128)(2,1)} %get-tuple-element.356) | copy-start | bytes 6291460 | tf_op jit(solution)/shard_map/while
  844.4 6.3 copy-start.4
  929.3 21.9 %copy-start.1 = (bf16[128,8192]{1,0:T(8,128)(2,1)S(1)}, bf16[128,8192]{1,0:T(8,128)(2,1)}, u32[]{:S(2)}) copy-start(bf16[128,8192]{1,0:T(8,128)(2,1)} %get-tuple-element.356) | copy-start | bytes 6291460 | tf_op jit(solution)/shard_map/while
  955.4 6.3 copy-start.4
  1040.2 21.9 %copy-start.1 = (bf16[128,8192]{1,0:T(8,128)(2,1)S(1)}, bf16[128,8192]{1,0:T(8,128)(2,1)}, u32[]{:S(2)}) copy-start(bf16[128,8192]{1,0:T(8,128)(2,1)} %get-tuple-element.356) | copy-start | bytes 6291460 | tf_op jit(solution)/shard_map/while
  1066.4 6.3 copy-start.4
  1151.2 21.9 %copy-start.1 = (bf16[128,8192]{1,0:T(8,128)(2,1)S(1)}, bf16[128,8192]{1,0:T(8,128)(2,1)}, u32[]{:S(2)}) copy-start(bf16[128,8192]{1,0:T(8,128)(2,1)} %get-tuple-element.356) | copy-start | bytes 6291460 | tf_op jit(solution)/shard_map/while
  1173.1 4.2 copy-start
  1177.4 6.3 copy-start.4
  1262.2 21.9 %copy-start.1 = (bf16[128,8192]{1,0:T(8,128)(2,1)S(1)}, bf16[128,8192]{1,0:T(8,128)(2,1)}, u32[]{:S(2)}) copy-start(bf16[128,8192]{1,0:T(8,128)(2,1)} %get-tuple-element.356) | copy-start | bytes 6291460 | tf_op jit(solution)/shard_map/while
  1288.3 6.3 copy-start.4
  1373.2 21.9 %copy-start.1 = (bf16[128,8192]{1,0:T(8,128)(2,1)S(1)}, bf16[128,8192]{1,0:T(8,128)(2,1)}, u32[]{:S(2)}) copy-start(bf16[128,8192]{1,0:T(8,128)(2,1)} %get-tuple-element.356) | copy-start | bytes 6291460 | tf_op jit(solution)/shard_map/while
  1399.3 6.3 copy-start.4
  1484.2 21.9 %copy-start.1 = (bf16[128,8192]{1,0:T(8,128)(2,1)S(1)}, bf16[128,8192]{1,0:T(8,128)(2,1)}, u32[]{:S(2)}) copy-start(bf16[128,8192]{1,0:T(8,128)(2,1)} %get-tuple-element.356) | copy-start | bytes 6291460 | tf_op jit(solution)/shard_map/while
  1510.3 6.3 copy-start.4
  1595.2 21.9 %copy-start.1 = (bf16[128,8192]{1,0:T(8,128)(2,1)S(1)}, bf16[128,8192]{1,0:T(8,128)(2,1)}, u32[]{:S(2)}) copy-start(bf16[128,8192]{1,0:T(8,128)(2,1)} %get-tuple-element.356) | copy-start | bytes 6291460 | tf_op jit(solution)/shard_map/while
  1617.0 4.2 copy-start
  1621.3 6.3 copy-start.4
  1706.2 21.9 %copy-start.1 = (bf16[128,8192]{1,0:T(8,128)(2,1)S(1)}, bf16[128,8192]{1,0:T(8,128)(2,1)}, u32[]{:S(2)}) copy-start(bf16[128,8192]{1,0:T(8,128)(2,1)} %get-tuple-element.356) | copy-start | bytes 6291460 | tf_op jit(solution)/shard_map/while
  1732.3 6.3 copy-start.4
  1817.1 21.9 %copy-start.1 = (bf16[128,8192]{1,0:T(8,128)(2,1)S(1)}, bf16[128,8192]{1,0:T(8,128)(2,1)}, u32[]{:S(2)}) copy-start(bf16[128,8192]{1,0:T(8,128)(2,1)} %get-tuple-element.356) | copy-start | bytes 6291460 | tf_op jit(solution)/shard_map/while
  1843.3 6.3 copy-start.4
  1884.9 97.1 %reduce-scatter.5.cloned.1.call-start = ((), (), s32[]{:S(2)}) async-start(), calls=%async_computation.7 | async-start | bytes 4718592 | tf_op jit(solution)/shard_map/reduce_scatter | solution.py:142
  (11 other events, 46.6 us)
Sparse Core Ops, SparseCore 0:
  9.5 30.6 all-gather.2
  42.2 32.8 all-gather.4
  1885.0 42.6 reduce-scatter.2
  1931.5 50.3 reduce-scatter.4
where the time goes:
time: 2020 us; the launch traced here: 1990 us
  local copies, waits for them, and re-layouts  1280 us (63%)
  matrix products  464 us (23%)
  waiting for transfers between devices  157 us (8%)
  other arithmetic  36.4 us (2%)
  blocking collectives  30.1 us (1%)
    dot_general x32, local copies, waits for them, and re-layouts, pair_update(): jnp.einsum('ahbk,hkc->abc', outer, weight_cube, preferred_element_type=jn...  365 us
    reshape x16, local copies, waits for them, and re-layouts, factor_pull(): return pulled.reshape(rows_i * hidden_dim, cols_j * hidden_dim)  350 us
    reshape x16, local copies, waits for them, and re-layouts, pair_update(): outer = outer.reshape(rows_i, hidden_dim, cols_j, hidden_dim)  276 us
    convert_element_type x16, local copies, waits for them, and re-layouts, factor_pull(): pulled = pulled.astype(jnp.bfloat16)  230 us
    dot_general x48, matrix products, dot_last(): lax.dot_general(left, right, (((1,), (1,)), ((), ())), preferred_element_...  144 us
    dot_general x16, matrix products, advance_sum(): jnp.dot(a_block, pulled, preferred_element_type=jnp.float32)  82.1 us
    dot_general x16, matrix products, dot_first(): lax.dot_general(left, right, (((0,), (0,)), ((), ())), preferred_element_...  78.1 us
    dot_general x16, matrix products, pair_update(): jnp.einsum('ahbk,hkc->abc', outer, weight_cube, preferred_element_type=jn...  58.5 us
  transfers between devices with their start and end apart: 5, of which 5 were waited for; matrix products, arithmetic and copies ran while one was open for 0% of the time, Pallas kernels for 0%

commit v1 on v0

v1 whole, which is shorter than its diff:
```python
import functools

import jax
import jax.numpy as jnp
from jax import lax
from jax.experimental import pallas as pl
from jax.experimental.pallas import tpu as pltpu
from jax.sharding import PartitionSpec as P

H = 32
F32 = jnp.float32
BF16 = jnp.bfloat16


def mm(left, right):
    return lax.dot_general(
        left, right, (((1,), (0,)), ((), ())), preferred_element_type=F32
    )


def mm_nt(left, right):
    return lax.dot_general(
        left, right, (((1,), (1,)), ((), ())), preferred_element_type=F32
    )


def pair_kernel(
    a_ref,
    b_ref,
    pair_ref,
    cot_ref,
    proj_t_ref,
    proj_ref,
    wide_ref,
    out_t_ref,
    in_ref,
    vec_ref,
    new_ref,
    grad_ref,
    ga_ref,
    gb_ref,
    outer_s,
    pulled_s,
    hidden_s,
    both_s,
    rhs_s,
    *,
    unit_chunk,
):
    seqs = a_ref.shape[0]
    rows, cols, width = pair_ref.shape
    units = out_t_ref.shape[1]
    inv_seqs = 1.0 / seqs

    @pl.when(pl.program_id(0) == 0)
    def _():
        gb_ref[...] = jnp.zeros_like(gb_ref)

    a_t = a_ref[...].T
    for h in range(H):
        outer = mm(a_t, b_ref[:, h * cols : (h + 1) * cols])
        outer_s[:, h * H : (h + 1) * H, :] = outer.astype(BF16).reshape(rows, H, cols)
    for i in range(rows):
        projected = mm(proj_t_ref[...], outer_s[i])
        updated = pair_ref[i].T.astype(F32) + (projected * inv_seqs + vec_ref[0])
        mean = jnp.mean(updated, axis=0, keepdims=True)
        centered = updated - mean
        var = jnp.mean(centered * centered, axis=0, keepdims=True)
        inv_std = lax.rsqrt(var + 1e-05)
        normed = centered * inv_std
        rhs_s[:width, :] = (normed * vec_ref[1] + vec_ref[2]).astype(BF16)
        rhs_s[width:, :] = cot_ref[i].T
        rhs = rhs_s[...]
        for u in range(0, units, unit_chunk):
            gate = mm(wide_ref[u : u + unit_chunk, :], rhs)
            up = mm(wide_ref[units + u : units + u + unit_chunk, :], rhs)
            d_hid = mm(wide_ref[2 * units + u : 2 * units + u + unit_chunk, :], rhs)
            sig = 0.5 * jnp.tanh(0.5 * gate) + 0.5
            act = gate * sig
            hidden_s[u : u + unit_chunk, :] = (act * up).astype(BF16)
            both_s[units + u : units + u + unit_chunk, :] = (d_hid * act).astype(BF16)
            both_s[u : u + unit_chunk, :] = (d_hid * up * (sig + act * (1.0 - sig))).astype(BF16)
        new_t = updated + mm(out_t_ref[...], hidden_s[...])
        new_ref[i] = new_t.astype(BF16).T
        d_norm = mm(in_ref[...], both_s[...]) * vec_ref[1]
        d_mean = jnp.mean(d_norm, axis=0, keepdims=True)
        d_proj = jnp.mean(d_norm * normed, axis=0, keepdims=True)
        grad_t = rhs_s[width:, :].astype(F32) + inv_std * (d_norm - d_mean - normed * d_proj)
        grad_t = grad_t.astype(BF16)
        grad_ref[i] = grad_t.T
        pulled_s[i] = mm(proj_ref[...], grad_t).astype(BF16)
    ga = jnp.zeros((rows * H, seqs), F32)
    for h in range(H):
        tile = pulled_s[:, h * H : (h + 1) * H, :].reshape(rows * H, cols)
        ga = ga + mm_nt(tile, b_ref[:, h * cols : (h + 1) * cols])
        gb_ref[:, h * cols : (h + 1) * cols] += mm(a_ref[...], tile)
    ga_ref[...] = ga.T


def pair_tile(a_own, b_cols, pair, cot, weights, block_rows, unit_chunk):
    seqs = a_own.shape[0]
    rows, cols, width = pair.shape
    units = weights[3].shape[1]

    def whole(array):
        return pl.BlockSpec(array.shape, lambda b: (0,) * array.ndim)

    pair_spec = pl.BlockSpec((block_rows, cols, width), lambda b: (b, 0, 0))
    a_spec = pl.BlockSpec((seqs, block_rows * H), lambda b: (0, b))
    return pl.pallas_call(
        functools.partial(pair_kernel, unit_chunk=unit_chunk),
        grid=(rows // block_rows,),
        in_specs=[a_spec, whole(b_cols), pair_spec, pair_spec] + [whole(w) for w in weights],
        out_specs=[pair_spec, pair_spec, a_spec, pl.BlockSpec((seqs, H * cols), lambda b: (0, 0))],
        out_shape=[
            jax.ShapeDtypeStruct((rows, cols, width), BF16),
            jax.ShapeDtypeStruct((rows, cols, width), BF16),
            jax.ShapeDtypeStruct((seqs, rows * H), F32),
            jax.ShapeDtypeStruct((seqs, H * cols), F32),
        ],
        scratch_shapes=[
            pltpu.VMEM((block_rows, H * H, cols), BF16),
            pltpu.VMEM((block_rows, H * H, cols), BF16),
            pltpu.VMEM((units, cols), BF16),
            pltpu.VMEM((2 * units, cols), BF16),
            pltpu.VMEM((2 * width, cols), BF16),
        ],
        compiler_params=pltpu.CompilerParams(
            dimension_semantics=("arbitrary",), vmem_limit_bytes=60 * 2**20
        ),
    )(a_own, b_cols, pair, cot, *weights)


def kernel_weights(proj_weight, proj_bias, norm_gain, norm_bias, trans_in, trans_out, cols):
    width = proj_weight.shape[1]
    units = trans_out.shape[0]
    proj = proj_weight.reshape(H, H, width).transpose(1, 0, 2).reshape(H * H, width)
    wide = jnp.concatenate(
        [
            jnp.concatenate([trans_in.T, jnp.zeros((2 * units, width), BF16)], axis=1),
            jnp.concatenate([jnp.zeros((units, width), BF16), trans_out], axis=1),
        ],
        axis=0,
    )
    vec = jnp.stack([proj_bias, norm_gain, norm_bias])[:, :, None]
    vec = jnp.broadcast_to(vec, (3, width, cols))
    return proj.T, proj, wide, trans_out.T, trans_in, vec


def body(
    factor_a,
    factor_b,
    pair,
    proj_weight,
    proj_bias,
    norm_gain,
    norm_bias,
    trans_in,
    trans_out,
    cotangent,
):
    rows_here, cols_here, width = pair.shape
    seqs_here = factor_a.shape[0]
    seq_count = seqs_here * lax.axis_size("row")
    cols = -(-cols_here // 128) * 128
    spare = cols - cols_here

    gathered = lax.all_gather(factor_a, "col", axis=1, tiled=True)
    a_own = lax.all_to_all(gathered, "row", split_axis=1, concat_axis=0, tiled=True)
    b_local = factor_b.reshape(seqs_here, cols_here, H).transpose(0, 2, 1)
    b_local = jnp.pad(b_local, ((0, 0), (0, 0), (0, spare))).reshape(seqs_here, H * cols)
    b_cols = lax.all_gather(b_local, "row", axis=0, tiled=True)
    if spare:
        pair = jnp.pad(pair, ((0, 0), (0, spare), (0, 0)))
        cotangent = jnp.pad(cotangent, ((0, 0), (0, spare), (0, 0)))
    weights = kernel_weights(
        proj_weight, proj_bias, norm_gain, norm_bias, trans_in, trans_out, cols
    )
    new_pair, pair_grad, ga_part, gb_part = pair_tile(
        a_own, b_cols, pair, cotangent, weights, 8, 128
    )
    new_pair = new_pair[:, :cols_here]
    pair_grad = pair_grad[:, :cols_here]
    gb_own = lax.psum_scatter(gb_part, "row", scatter_dimension=0, tiled=True)
    gb_own = gb_own.reshape(seqs_here, H, cols)[:, :, :cols_here].transpose(0, 2, 1)
    grad_b = gb_own.reshape(seqs_here, cols_here * H) / seq_count
    returned = lax.all_to_all(ga_part, "row", split_axis=0, concat_axis=1, tiled=True)
    grad_a = lax.psum_scatter(returned, "col", scatter_dimension=1, tiled=True) / seq_count
    return (new_pair, pair_grad, grad_a, grad_b)


def solution(mesh):
    placed = (
        P("row", "col"),
        P("row", "col"),
        P("row", "col", None),
        P(),
        P(),
        P(),
        P(),
        P(),
        P(),
        P("row", "col", None),
    )
    return jax.shard_map(
        body,
        mesh=mesh,
        in_specs=placed,
        out_specs=(P("row", "col", None), P("row", "col", None), P("row", "col"), P("row", "col")),
        check_vma=False,
    )
```

time: 2020 us -> 404 us (0.20); the launches traced: 1990 us -> 404 us
  local copies, waits for them, and re-layouts: 1280 us -> 11.9 us
  matrix products: 464 us -> 0 us
  Pallas kernels: 0 us -> 189 us
  other arithmetic: 36.4 us -> 3.92 us
    reshape x32 -> x2, local copies, waits for them, and re-layouts: 626 us -> 1.81 us  [the longest x1 1.71 us: body(): b_local = factor_b.reshape(seqs_here, cols_here, H).transpose(0, 2, 1)]
    dot_general x144 -> x0, matrix products: 464 us -> none  [the longest x48 144 us: dot_last(): lax.dot_general(left, right, (((1,), (1,)), ((), ())), preferred_element_...]
    dot_general x32 -> x0, local copies, waits for them, and re-layouts: 365 us -> none  [pair_update(): jnp.einsum('ahbk,hkc->abc', outer, weight_cube, preferred_element_type=jn...]
    convert_element_type x16 -> x0, local copies, waits for them, and re-layouts: 230 us -> none  [factor_pull(): pulled = pulled.astype(jnp.bfloat16)]
    pallas_call x0 -> x1, Pallas kernels: none -> 189 us  [pair_tile(): pl.pallas_call(functools.partial(pair_kernel, unit_chunk=unit_chunk), gri...]
    dynamic_slice x32 -> x0, local copies, waits for them, and re-layouts: 34.5 us -> none  [body(): lax.scan(advance_sum, start_sum, (a_blocks, pair_blocks, cot_blocks))]
    convert_element_type x16 -> x0, other arithmetic: 26 us -> none  [pair_update(): grad_rows = grad_flat.astype(jnp.bfloat16).reshape(rows_i, cols_j, width)]
  transfers between devices with their start and end apart: 5 -> 5, of which waited for: 5 -> 5; matrix products, arithmetic and copies ran while one was open for 0% -> 2% of each run, Pallas kernels for 0% -> 0%
where the time goes in v1:
time: 404 us
  Pallas kernels  189 us (47%)
  waiting for transfers between devices  151 us (37%)
  blocking collectives  30.1 us (7%)
  between operations  13.9 us (3%)
  local copies, waits for them, and re-layouts  11.9 us (3%)
    pallas_call x1, Pallas kernels, pair_tile(): pl.pallas_call(functools.partial(pair_kernel, unit_chunk=unit_chunk), gri...  189 us
    reduce_scatter x1, waiting for transfers between devices, body(): gb_own = lax.psum_scatter(gb_part, 'row', scatter_dimension=0, tiled=True)  51.7 us
    reduce_scatter x1, waiting for transfers between devices, body(): lax.psum_scatter(returned, 'col', scatter_dimension=1, tiled=True)  42.3 us
    all_to_all x1, blocking collectives, body(): lax.all_to_all(ga_part, 'row', split_axis=0, concat_axis=1, tiled=True)  30.1 us
    all_gather x1, waiting for transfers between devices, body(): gathered = lax.all_gather(factor_a, 'col', axis=1, tiled=True)  29.5 us
    all_to_all x1, waiting for transfers between devices, body(): lax.all_to_all(gathered, 'row', split_axis=1, concat_axis=0, tiled=True)  15.2 us
    all_gather x1, waiting for transfers between devices, body(): b_cols = lax.all_gather(b_local, 'row', axis=0, tiled=True)  11.1 us
  transfers between devices with their start and end apart: 5, of which 5 were waited for; matrix products, arithmetic and copies ran while one was open for 2% of the time, Pallas kernels for 0%

profile of v1, /device:TPU:0, one launch (start us, length us, event | category | flops | bytes accessed | tf_op | source)
XLA Modules:
  0.0 403.5 jit_solution(13406009226446252015)
XLA Ops:
  7.2 0.0 all-gather.3.cloned.1.call-start
  7.2 0.7 all-gather.3.cloned.1.call-update
  7.9 0.0 all-gather.5.cloned.1.call-start
  7.9 1.7 reshape.33
  9.7 1.1 copy.40
  10.8 0.0 all-gather.5.cloned.1.call-update
  10.8 29.5 %all-gather.3.cloned.1.call-done = bf16[16,32768]{1,0:T(8,128)(2,1)} async-done(((bf16[16,8192]{1,0:T(8,128)(2,1)}), bf16[16,32768]{1,0:T(8,128)(2,1)}) %all-gather.3.cloned.1.call-update) | async-done | bytes 1048592 | tf_op jit(solution)/shard_map/all_gather | solution.py:168
  40.3 0.0 copy-start.3
  40.3 0.0 copy-start.4
  40.3 2.3 copy.44
  42.6 0.0 copy-start.2
  42.6 0.0 copy-start.5
  42.6 0.0 copy-start.6
  42.6 0.0 copy-start.7
  42.6 3.8 all-to-all-start
  46.4 0.0 reduce-scatter.3.cloned.1.call-start
  46.5 0.0 copy-done.3
  46.5 0.8 copy.34
  47.3 0.0 copy-done.4
  47.3 0.1 copy.32
  47.4 0.0 copy-start.1
  47.4 0.9 copy.35.proj_t_ref
  48.2 0.0 copy-done.2
  48.2 0.2 copy.33
  48.4 0.0 copy-done.5
  48.4 0.0 copy-done.6
  48.4 0.0 copy-done.7
  48.5 1.0 fusion.2.wide_ref
  49.4 15.2 %all-to-all-done = bf16[16,8,4096]{2,0,1:T(8,128)(2,1)S(1)} async-done(((bf16[16,8,4096]{2,0,1:T(8,128)(2,1)}), bf16[16,8,4096]{2,0,1:T(8,128)(2,1)S(1)}, u32[]{:S(2)}, u32[]{:S(2)}) %all-to-all-start) | async-done | bytes 1048608 | tf_op jit(solution)/shard_map/all_to_all | solution.py:169
  64.6 0.0 copy-start
  64.6 11.1 %all-gather.5.cloned.1.call-done.b_ref = bf16[128,8192]{1,0:T(8,128)(2,1)} async-done(((bf16[16,8192]{1,0:T(8,128)(2,1)}), bf16[128,8192]{1,0:T(8,128)(2,1)}) %all-gather.5.cloned.1.call-update) | async-done | bytes 2097168 | tf_op jit(solution)/shard_map/all_gather | solution.py:172
  75.6 0.9 broadcast_in_dim.2.vec_ref
  76.5 0.0 copy-done.1
  76.5 0.0 copy-done
  76.5 188.8 %shard_map.129 = (bf16[128,256,128]{2,1,0:T(8,128)(2,1)}, bf16[128,256,128]{2,1,0:T(8,128)(2,1)}, f32[128,4096]{1,0:T(8,128)}, f32[128,8192]{1,0:T(8,128)}) custom-call(bf16[128,4096]{1,0:T(8,128)(2,1)} %bitcast.34, bf16[128,8192]{1,0:T(8,128)(2,1)} %all-gather.5.cloned.1.call-done.b_ref, bf16[128,256,128]{2,1,0:T(8,128)(2,1)} %pair_ref.1, ...), custom_call_target="tpu_custom_call" | custom-call | tf_op jit(solution)/shard_map/pallas_call | solution.py:110
  265.3 30.1 %all_to_all.38 = f32[8,16,4096]{2,1,0:T(8,128)S(1)} all-to-all(f32[8,16,4096]{2,1,0:T(8,128)} %bitcast.38), channel_id=1, replica_groups=mesh['row'=8,'col'=4] {'row'}, dimensions={0} | all-to-all | bytes 4194304 | tf_op jit(solution)/shard_map/all_to_all | solution.py:187
  295.4 1.5 copy.39
  296.9 0.0 reduce-scatter.3.cloned.1.call-update
  296.9 0.0 reduce-scatter.5.cloned.1.call-start
  297.0 0.5 reduce-scatter.5.cloned.1.call-update
  297.5 42.3 %reduce-scatter.3.cloned.1.call-done = f32[16,8192]{1,0:T(8,128)} async-done(((f32[16,32768]{1,0:T(8,128)}), f32[16,8192]{1,0:T(8,128)}) %reduce-scatter.3.cloned.1.call-update) | async-done | bytes 524304 | tf_op jit(solution)/shard_map/reduce_scatter | solution.py:188
  339.8 1.9 broadcast_multiply_fusion.1
  341.7 51.7 %reduce-scatter.5.cloned.1.call-done = f32[16,8192]{1,0:T(8,128)} async-done(((f32[128,8192]{1,0:T(8,128)}), f32[16,8192]{1,0:T(8,128)}) %reduce-scatter.5.cloned.1.call-update) | async-done | bytes 524304 | tf_op jit(solution)/shard_map/reduce_scatter | solution.py:184
  393.4 1.1 broadcast_multiply_fusion
  394.5 0.2 copy.41
  394.7 0.6 copy.37
  395.3 1.8 div.16
  (1 shorter events, 0.0 us)
Async XLA Ops:
  7.2 33.1 %all-gather.3.cloned.1.call-start = ((), (), s32[]{:S(2)}) async-start(), calls=%async_computation.4 | async-start | bytes 1310720 | tf_op jit(solution)/shard_map/all_gather | solution.py:168
  7.9 67.7 %all-gather.5.cloned.1.call-start = ((), (), s32[]{:S(2)}) async-start(), calls=%async_computation.5 | async-start | bytes 2359296 | tf_op jit(solution)/shard_map/all_gather | solution.py:172
  40.3 6.2 %copy-start.3 = (bf16[512,128]{1,0:T(8,128)(2,1)S(1)}, bf16[512,128]{1,0:T(8,128)(2,1)}, u32[]{:S(2)}) copy-start(bf16[512,128]{1,0:T(8,128)(2,1)} %param.18) | copy-start | bytes 393220
  40.3 7.0 %copy-start.4 = (bf16[1024,128]{1,0:T(8,128)(2,1)S(1)}, bf16[1024,128]{1,0:T(8,128)(2,1)}, u32[]{:S(2)}) copy-start(bf16[1024,128]{1,0:T(8,128)(2,1)} %param.13) | copy-start | bytes 786436
  42.6 5.6 %copy-start.2 = (bf16[128,1024]{1,0:T(8,128)(2,1)S(1)}, bf16[128,1024]{1,0:T(8,128)(2,1)}, u32[]{:S(2)}) copy-start(bf16[128,1024]{1,0:T(8,128)(2,1)} %in_ref.1) | copy-start | bytes 786436
  42.6 5.8 %copy-start.5 = (f32[128]{0:T(128)S(1)}, f32[128]{0:T(128)}, u32[]{:S(2)}) copy-start(f32[128]{0:T(128)} %param.16) | copy-start | bytes 1540
  42.6 5.8 %copy-start.6 = (f32[128]{0:T(128)S(1)}, f32[128]{0:T(128)}, u32[]{:S(2)}) copy-start(f32[128]{0:T(128)} %param.15) | copy-start | bytes 1540
  42.6 5.8 %copy-start.7 = (f32[128]{0:T(128)S(1)}, f32[128]{0:T(128)}, u32[]{:S(2)}) copy-start(f32[128]{0:T(128)} %param.14) | copy-start | bytes 1540
  42.6 21.9 %all-to-all-start = ((bf16[16,8,4096]{2,0,1:T(8,128)(2,1)}), bf16[16,8,4096]{2,0,1:T(8,128)(2,1)S(1)}, u32[]{:S(2)}, u32[]{:S(2)}) async-start(bf16[16,8,4096]{2,0,1:T(8,128)(2,1)} %bitcast.29), calls=%async_computation | async-start | bytes 2097152 | tf_op jit(solution)/shard_map/all_to_all | solution.py:169
  46.4 293.4 %reduce-scatter.3.cloned.1.call-start = ((), (), s32[]{:S(2)}) async-start(), calls=%async_computation.6 | async-start | bytes 2621440 | tf_op jit(solution)/shard_map/reduce_scatter | solution.py:188
  47.4 29.1 %copy-start.1 = (bf16[32,32,128]{2,0,1:T(8,128)(2,1)}, bf16[32,32,128]{2,0,1:T(8,128)(2,1)S(1)}, u32[]{:S(2)}) copy-start(bf16[32,32,128]{2,0,1:T(8,128)(2,1)S(1)} %copy.32) | copy-start | bytes 786436
  64.6 11.9 %copy-start = (bf16[16,8,4096]{2,0,1:T(8,128)(2,1)}, bf16[16,8,4096]{2,0,1:T(8,128)(2,1)S(1)}, u32[]{:S(2)}) copy-start(bf16[16,8,4096]{2,0,1:T(8,128)(2,1)S(1)} %all-to-all-done) | copy-start | bytes 3145732
  296.9 96.5 %reduce-scatter.5.cloned.1.call-start = ((), (), s32[]{:S(2)}) async-start(), calls=%async_computation.7 | async-start | bytes 4718592 | tf_op jit(solution)/shard_map/reduce_scatter | solution.py:184
Sparse Core Ops, SparseCore 0:
  9.5 30.6 all-gather.2
  42.7 32.8 all-gather.4
  297.0 42.7 reduce-scatter.2
  343.0 50.3 reduce-scatter.4
